TPU v7x, 32 devices: a whole 2x2x4 slice. The times are simulated.
32 devices in a mesh: wrow: 4 (over y, core), wcol: 2 (over x), dom: 4 (over z).
Axes of the slice: x: 2, y: 2, z: 4, core: 2. Of those that a mesh axis runs over, the one named last changes fastest.
Arguments:
- positions: float32 [4, 2, 3, 8192], P('wrow', 'wcol', None, 'dom'), may hold values from -6 to 6
- velocities: float32 [4, 2, 3, 8192], P('wrow', 'wcol', None, 'dom'), may hold values from -6 to 6
- inv_mass: float32 [8192], P('dom'), may hold values from 0.5 to 2
- cv_weight: float32 [2, 3, 8192], P(None, None, 'dom'), may hold values from -0.125 to 0.125
- stiffness: float32 [2], replicated, may hold values from 1 to 4
- centers: float32 [4, 2, 2], P('wrow', 'wcol'), may hold values from -3 to 3
- block_order: int32 [8192], P('dom'), may hold values from 0 to 2047, as said below
- pair_count: int32 [4], P('dom'), may hold values from 16 to 64, as said below
- pair_own: int32 [4, 64], P('dom'), may hold values from 0 to 15, as said below
- pair_other: int32 [4, 64], P('dom'), may hold values from 0 to 47, as said below
- accept_row: int32 [4, 2], P('wrow', 'wcol'), may hold values from 0 to 1, as said below
- accept_col: int32 [4, 2], P('wrow', 'wcol'), may hold values from 0 to 1, as said below
Outputs:
- new_positions: float32 [4, 2, 3, 8192], P('wrow', 'wcol', None, 'dom')
- new_velocities: float32 [4, 2, 3, 8192], P('wrow', 'wcol', None, 'dom')
- new_forces: float32 [4, 2, 3, 8192], P('wrow', 'wcol', None, 'dom')
Inputs may be any that keep to these rules, and one draw needn't show every extreme that they name: accept_row is equal for windows (2k, c) and (2k + 1, c). accept_col is equal for windows (r, 2k) and (r, 2k + 1). `block_order`: each slab's 2048 entries are a permutation of 0 to 2047. `pair_count`: some slab has exactly 64 live pairs. `pair_own`: entries past the slab's pair_count are 0. `pair_other`: slab 0 names no lower slab and the last slab no upper slab; entries past the slab's pair_count are 16.
All inputs are finite; a program needn't handle non-finite values.
Results may differ from a plain program's by a relative error of at most 0.0003.
Values sent between devices are 32-bit elements; how exact they have to be, the bound alone decides.
A program may use at most 64 MiB of HBM per device.

v0:
```python
import functools
import math

import numpy as np
import jax
import jax.numpy as jnp
from jax import lax
from jax.experimental import pallas as pl
from jax.experimental.pallas import tpu as pltpu
from jax.sharding import PartitionSpec as P

BLK = 128
STEPS = 3
PAIR_EPS = 0.015625
DT = 0.1
SCALE = math.sqrt(math.log2(math.e))
ROWS = 32
UNROLL = 16
OTHER_ROWS = {0: 0, 1: 1, 2: 2, 3: 3, 4: 4, 5: 5, 6: 9, 7: 9, 8: 9, 9: 6, 10: 7, 11: 8, 16: 0, 17: 1, 18: 2, 19: 3, 20: 4, 21: 5}
OWN_ROWS = {0: 0, 1: 1, 2: 2, 3: 0, 4: 1, 5: 2, 6: 6, 7: 7, 8: 8, 9: 9, 10: 9, 11: 9, 16: 3, 17: 4, 18: 5, 19: 3, 20: 4, 21: 5}
MESH = pl.DeviceIdType.MESH
F32 = jnp.float32
BF16 = jnp.bfloat16


def split3(value):
    high = value.astype(BF16)
    rest = value - high.astype(F32)
    middle = rest.astype(BF16)
    low = (rest - middle.astype(F32)).astype(BF16)
    return high, middle, low


def stacked_split(value):
    return jnp.concatenate(split3(value), axis=0)


def unsplit(value, rows):
    return value[0:rows] + (value[rows : 2 * rows] + value[2 * rows : 3 * rows])


def placing(rows_of, nb):
    table = np.zeros((nb, ROWS, 10, nb), np.float32)
    for row, kind in rows_of.items():
        for b in range(nb):
            table[b, row, kind, b] = 1.0
    return jnp.asarray(table.reshape(nb * ROWS, 10 * nb), BF16)


def kernel(
    sizes,
    pos, vel, mass, cvw, order, own_row, place_own, place_other, own_s, other_s, count_s, stiff_s, centers_s, arow_s, acol_s,
    out_x, out_v, out_f,
    onehot, high_block, raw, raw_w, got_x, got_v, got_aux, aux, parts, tiles, others_of, turned_own, summing, xs, vs, fs, ms, ws,
    sx_send, sx_recv, sv_send, sv_recv, sa_send, sa_recv, halo_send, halo_recv, part_send, part_recv, *nears,
):
    doms, nb, slots = sizes
    row = lax.axis_index("wrow")
    col = lax.axis_index("wcol")
    me = lax.axis_index("dom")
    row_to = row + 1 - 2 * lax.rem(row, 2)
    col_to = col + 1 - 2 * lax.rem(col, 2)
    partners = [(row_to, col, me), (row, col_to, me), (row_to, col_to, me)]
    others = [(row, col, lax.rem(me + off, doms)) for off in range(1, doms)]

    lines = lax.broadcasted_iota(jnp.int32, (8, BLK), 0)
    aux[...] = jnp.where(
        lines == 0,
        centers_s[0, 0],
        jnp.where(lines == 1, centers_s[0, 1], arow_s[0, 0].astype(F32)),
    )
    for held in nears:
        held[...] = jnp.zeros(held.shape, F32)
    barrier = pltpu.get_barrier_semaphore()
    for target in partners + others:
        pl.semaphore_signal(barrier, inc=1, device_id=target, device_id_type=MESH)
    pl.semaphore_wait(barrier, len(partners) + len(others))

    def exchange(source, target, sends, recvs):
        copies = []
        for at, partner in enumerate(partners):
            copy = pltpu.make_async_remote_copy(
                src_ref=source,
                dst_ref=target.at[at],
                send_sem=sends.at[at],
                recv_sem=recvs.at[at],
                device_id=partner,
                device_id_type=MESH,
            )
            copy.start()
            copies.append(copy)
        return copies

    aux_copies = exchange(aux, got_aux, sa_send, sa_recv)
    x_copies = exchange(pos, got_x, sx_send, sx_recv)
    v_copies = exchange(vel, got_v, sv_send, sv_recv)

    jl = lax.broadcasted_iota(jnp.int32, (BLK, BLK), 0)
    listed = order[...]
    low = lax.rem(listed, BLK)
    high_block[...] = lax.div(listed, BLK)
    for b in range(nb):
        onehot[:, b * BLK : (b + 1) * BLK] = jnp.where(low[b : b + 1, :] == jl, 1.0, 0.0).astype(BF16)
    jb_lines = lax.broadcasted_iota(jnp.int32, (nb, BLK), 0)

    def permuted(source, comps, store):
        split = stacked_split(source)

        def body(b, carry):
            at = pl.ds(pl.multiple_of(b * BLK, BLK), BLK)
            picked = jnp.dot(split, onehot[:, at], preferred_element_type=F32)
            picked = unsplit(picked, comps * nb)
            mask = high_block[pl.ds(b, 1), :] == jb_lines
            for k in range(comps):
                line = jnp.sum(jnp.where(mask, picked[k * nb : (k + 1) * nb], 0.0), axis=0, keepdims=True)
                store(k, b, line)
            return carry

        lax.fori_loop(0, nb, body, 0, unroll=True)

    def unpermuted(source_ref):
        def body(b, total):
            at = pl.ds(pl.multiple_of(b * BLK, BLK), BLK)
            mask = high_block[pl.ds(b, 1), :] == jb_lines
            spread = jnp.concatenate(
                [jnp.where(mask, source_ref[k, pl.ds(b, 1), :], 0.0) for k in range(3)], axis=0
            )
            return total + lax.dot_general(
                stacked_split(spread), onehot[:, at], (((1,), (1,)), ((), ())), preferred_element_type=F32
            )

        total = lax.fori_loop(0, nb, body, jnp.zeros((9 * nb, BLK), F32), unroll=True)
        return unsplit(total, 3 * nb).reshape(3, nb, BLK)

    for b in range(nb):
        at = slice(b * BLK, (b + 1) * BLK)
        for k in range(2):
            for c in range(3):
                raw_w[(3 * k + c) * nb + b : (3 * k + c) * nb + b + 1, :] = cvw[k, c : c + 1, at]
    raw_w[6 * nb : 7 * nb, :] = mass[...]

    def store_w(k, b, line):
        if k < 6:
            ws[k // 3, k % 3, pl.ds(b, 1), :] = line
        else:
            ms[pl.ds(b, 1), :] = line

    permuted(raw_w[...], 7, store_w)

    wide = 8 * slots
    at_slot = lax.div(lax.broadcasted_iota(jnp.int32, (slots, wide), 1), 8)
    spread_slots = jnp.where(at_slot == lax.broadcasted_iota(jnp.int32, (slots, wide), 0), 1.0, 0.0).astype(BF16)
    live = lax.broadcasted_iota(jnp.int32, (8, slots), 1) < count_s[0]
    owners = jnp.where(live, jnp.broadcast_to(own_row[...], (8, slots)).astype(F32), -1.0).astype(BF16)
    owners = jnp.dot(owners, spread_slots, preferred_element_type=F32)[0:1, :]
    block_line = lax.broadcasted_iota(jnp.int32, (nb, wide), 0).astype(F32)
    row_line = lax.rem(lax.broadcasted_iota(jnp.int32, (nb, wide), 1), 8)
    for r in range(7):
        summing[r * nb : (r + 1) * nb, :] = jnp.where(
            (owners == block_line) & (row_line == r), 1.0, 0.0
        ).astype(BF16)

    for copy in aux_copies:
        copy.wait()
    take_row = jnp.full((8, BLK), arow_s[0, 0].astype(F32)) > 0.5
    take_col = jnp.full((8, BLK), acol_s[0, 0].astype(F32)) > 0.5
    take_far = jnp.broadcast_to(got_aux[1, 2:3, :], (8, BLK)) > 0.5

    def chosen(mine, by_row, by_col, by_both):
        far = jnp.where(take_far, by_both, by_col)
        close = jnp.where(take_row, by_row, mine)
        return jnp.where(take_col, far, close)

    centre = chosen(aux[...], got_aux[0], got_aux[1], got_aux[2])
    centres = [centre[0:1, :], centre[1:2, :]]

    def take_window(source, got):
        for c in range(3):
            for b in range(0, nb, 8):
                raw[c * nb + b : c * nb + b + 8, :] = chosen(
                    source[c, b : b + 8], got[0, c, b : b + 8], got[1, c, b : b + 8], got[2, c, b : b + 8]
                )

    for copy in x_copies:
        copy.wait()
    take_window(pos, got_x)

    def store_x(k, b, line):
        xs[k, pl.ds(b, 1), :] = line

    def store_v(k, b, line):
        vs[k, pl.ds(b, 1), :] = line

    permuted(raw[...], 3, store_x)

    def take_velocities():
        for copy in v_copies:
            copy.wait()
        take_window(vel, got_v)
        permuted(raw[...], 3, store_v)

    def force(e, meanwhile):
        near = nears[e]
        x = xs[...]
        near[1] = x * SCALE
        up = pltpu.make_async_remote_copy(
            src_ref=near.at[1],
            dst_ref=near.at[0],
            send_sem=halo_send.at[e, 0],
            recv_sem=halo_recv.at[e, 0],
            device_id=(row, col, lax.rem(me + 1, doms)),
            device_id_type=MESH,
        )
        down = pltpu.make_async_remote_copy(
            src_ref=near.at[1],
            dst_ref=near.at[2],
            send_sem=halo_send.at[e, 1],
            recv_sem=halo_recv.at[e, 1],
            device_id=(row, col, lax.rem(me + doms - 1, doms)),
            device_id_type=MESH,
        )

        @pl.when(me < doms - 1)
        def _():
            up.start()

        @pl.when(me > 0)
        def _():
            down.start()

        for k in range(2):
            part = jnp.sum(ws[k] * x, axis=0)
            parts[e, me, k] = jnp.sum(part.reshape(nb // 8, 8, BLK), axis=0)
        part_copies = []
        for at, target in enumerate(others):
            copy = pltpu.make_async_remote_copy(
                src_ref=parts.at[e, me],
                dst_ref=parts.at[e, me],
                send_sem=part_send.at[e, at],
                recv_sem=part_recv.at[e, at],
                device_id=target,
                device_id_type=MESH,
            )
            copy.start()
            part_copies.append(copy)

        def features(slab):
            highs, middles, held = [], [], []
            for k in range(3):
                value = near[slab, k]
                high = value.astype(BF16)
                middle = (value - high.astype(F32)).astype(BF16)
                highs.append(high)
                middles.append(middle)
                held.append(high.astype(F32) + middle.astype(F32))
            norm = -0.5 * (held[0] * held[0] + held[1] * held[1] + held[2] * held[2])
            ones = jnp.ones((nb, BLK), BF16)
            return jnp.concatenate(highs + middles + list(split3(norm)) + [ones], axis=0), held

        def place_others(slab, kinds):
            placed = jnp.dot(place_other[...], kinds, preferred_element_type=F32).astype(BF16)
            others_of[slab * nb : (slab + 1) * nb] = placed.reshape(nb, ROWS, BLK)

        kinds, held = features(1)
        place_others(1, kinds)
        placed = jnp.dot(place_own[...], kinds, preferred_element_type=F32)
        for b in range(nb):
            turned_own[b] = jnp.transpose(placed[b * ROWS : (b + 1) * ROWS]).astype(BF16)

        meanwhile()

        @pl.when(me < doms - 1)
        def _():
            up.wait_send()
            down.wait_recv()

        @pl.when(me > 0)
        def _():
            down.wait_send()
            up.wait_recv()

        place_others(0, features(0)[0])
        place_others(2, features(2)[0])

        def slots_at(first):
            for p in [first + u for u in range(UNROLL)]:
                theirs = others_of[other_s[0, p]]
                weight = jnp.exp2(jnp.dot(turned_own[own_s[0, p]], theirs, preferred_element_type=F32))
                high = weight.astype(BF16)
                low = (weight - high.astype(F32)).astype(BF16)
                lines_of = theirs[0:16, :]
                pulled = lax.dot_general(
                    jnp.concatenate([lines_of, lines_of], axis=1),
                    jnp.concatenate([high, low], axis=1),
                    (((1,), (1,)), ((), ())),
                    preferred_element_type=F32,
                )
                tiles[p] = pulled[0:8, :]

        def body(i, carry):
            slots_at(i * UNROLL)
            return carry

        lax.fori_loop(0, slots // UNROLL, body, 0)

        for copy in part_copies:
            copy.wait()
        sums = parts[e, 0]
        for d in range(1, doms):
            sums = sums + parts[e, d]
        pulls = []
        for k in range(2):
            collective = jnp.sum(sums[k], axis=(0, 1), keepdims=True)
            pulls.append(stiff_s[k] * (collective - centres[k]))
        total = sum(
            jnp.dot(summing[...], term, preferred_element_type=F32)
            for term in split3(tiles[...].reshape(8 * slots, BLK))[::-1]
        )
        for k in range(3):
            pulled = total[k * nb : (k + 1) * nb] + total[(3 + k) * nb : (4 + k) * nb]
            pair = held[k] * total[6 * nb : 7 * nb] - pulled
            fs[k] = (PAIR_EPS / SCALE) * pair - pulls[0] * ws[0, k] - pulls[1] * ws[1, k]

    force(0, take_velocities)
    for step in range(STEPS):
        half = 0.5 * DT * ms[...]
        for k in range(3):
            v = vs[k] + half * fs[k]
            vs[k] = v
            xs[k] = xs[k] + DT * v
        if step < STEPS - 1:
            force(step + 1, lambda: None)
            for k in range(3):
                vs[k] = vs[k] + half * fs[k]

    def write_positions():
        out_x[...] = unpermuted(xs)
        out_v[...] = unpermuted(vs)

    force(STEPS, write_positions)
    forces = unpermuted(fs)
    out_f[...] = forces
    out_v[...] = out_v[...] + (0.5 * DT) * mass[...][None] * forces


def per_device(
    positions, velocities, inv_mass, cv_weight, stiffness, centers, block_order, pair_count, pair_own, pair_other,
    accept_row, accept_col,
):
    atoms = block_order.shape[0]
    nb = atoms // BLK
    slots = pair_own.shape[1]
    doms = lax.axis_size("dom")
    evals = STEPS + 1
    vmem = pl.BlockSpec(memory_space=pltpu.VMEM)
    smem = pl.BlockSpec(memory_space=pltpu.SMEM)
    dma = pltpu.SemaphoreType.DMA
    shape = jax.ShapeDtypeStruct((3, nb, BLK), F32)
    outs = pl.pallas_call(
        functools.partial(kernel, (doms, nb, slots)),
        out_shape=(shape, shape, shape),
        in_specs=[vmem] * 8 + [smem] * 7,
        out_specs=(vmem, vmem, vmem),
        scratch_shapes=[
            pltpu.VMEM((BLK, atoms), BF16),
            pltpu.VMEM((nb, BLK), jnp.int32),
            pltpu.VMEM((3 * nb, BLK), F32),
            pltpu.VMEM((7 * nb, BLK), F32),
            pltpu.VMEM((3, 3, nb, BLK), F32),
            pltpu.VMEM((3, 3, nb, BLK), F32),
            pltpu.VMEM((3, 8, BLK), F32),
            pltpu.VMEM((8, BLK), F32),
            pltpu.VMEM((evals, doms, 2, 8, BLK), F32),
            pltpu.VMEM((slots, 8, BLK), F32),
            pltpu.VMEM((3 * nb, ROWS, BLK), BF16),
            pltpu.VMEM((nb, BLK, ROWS), BF16),
            pltpu.VMEM((7 * nb, 8 * slots), BF16),
            pltpu.VMEM((3, nb, BLK), F32),
            pltpu.VMEM((3, nb, BLK), F32),
            pltpu.VMEM((3, nb, BLK), F32),
            pltpu.VMEM((nb, BLK), F32),
            pltpu.VMEM((2, 3, nb, BLK), F32),
            dma((3,)), dma((3,)), dma((3,)), dma((3,)), dma((3,)), dma((3,)),
            dma((evals, 2)), dma((evals, 2)), dma((evals, doms)), dma((evals, doms)),
        ]
        + [pltpu.VMEM((3, 3, nb, BLK), F32)] * evals,
        compiler_params=pltpu.CompilerParams(collective_id=0, has_side_effects=True),
        name="windows",
    )(
        positions.reshape(3, nb, BLK), velocities.reshape(3, nb, BLK), inv_mass.reshape(nb, BLK), cv_weight, block_order.reshape(nb, BLK), pair_own,
        placing(OWN_ROWS, nb), placing(OTHER_ROWS, nb), pair_own, pair_other, pair_count, stiffness, centers[0], accept_row, accept_col,
    )
    return tuple(out.reshape(1, 1, 3, atoms) for out in outs)


def solution(mesh):
    placed = (
        P("wrow", "wcol", None, "dom"),
        P("wrow", "wcol", None, "dom"),
        P("dom"),
        P(None, None, "dom"),
        P(),
        P("wrow", "wcol", None),
        P("dom"),
        P("dom"),
        P("dom", None),
        P("dom", None),
        P("wrow", "wcol"),
        P("wrow", "wcol"),
    )
    return jax.shard_map(
        per_device,
        mesh=mesh,
        in_specs=placed,
        out_specs=(
            P("wrow", "wcol", None, "dom"),
            P("wrow", "wcol", None, "dom"),
            P("wrow", "wcol", None, "dom"),
        ),
        check_vma=False,
    )
```

profile of v0, /device:TPU:0, one launch (start us, length us, event | category | flops | bytes accessed | tf_op | source)
XLA Modules:
  0.0 56.3 jit_solution(6714918223167324676)
XLA Ops:
  2.6 1.4 %copy.21.cvw = f32[2,3,2048]{2,1,0:T(4,128)} copy(f32[2,3,2048]{2,0,1:T(2,128)} %param.17) | data formatting | bytes 98304 | tf_op args[3]
  4.0 49.6 %windows.1 = (f32[3,16,128]{2,1,0:T(8,128)}, f32[3,16,128]{2,1,0:T(8,128)}, f32[3,16,128]{2,1,0:T(8,128)}) custom-call(f32[3,16,128]{2,1,0:T(8,128)} %bitcast.8, f32[3,16,128]{2,1,0:T(8,128)} %bitcast.9, f32[16,128]{1,0:T(8,128)} %bitcast.13, f32[2,3,2048]{2,1,0:T(4,128)} %copy.21.cvw, s32[16,128]{1,0:T(8,128)} %bitcast.14, s32[1,64]{1,0:T(1,128)} %own_s.1, ...), custom_call_target="tpu_custom_call" | custom-call | tf_op jit(solution)/shard_map/windows/pallas_call | solution.py:359
  53.6 0.0 copy-start.1
  53.6 1.4 %copy.31 = f32[1,1,3,2048]{3,1,2,0:T(1,128)} copy(f32[1,1,3,2048]{3,1,2,0:T(1,128)} %bitcast.12) | data formatting | bytes 49152
  55.0 0.0 copy-done.1
  55.0 0.0 copy-start
  55.0 0.6 %copy.32 = f32[1,1,3,2048]{3,1,2,0:T(1,128)} copy(f32[1,1,3,2048]{3,1,2,0:T(1,128)S(1)} %bitcast.11) | data formatting | bytes 49152
  55.6 0.1 copy-done
  55.7 0.6 %copy.33 = f32[1,1,3,2048]{3,1,2,0:T(1,128)} copy(f32[1,1,3,2048]{3,1,2,0:T(1,128)S(1)} %bitcast.10) | data formatting | bytes 49152
Async XLA Ops:
  53.6 1.4 %copy-start.1 = (f32[3,16,128]{2,1,0:T(8,128)S(1)}, f32[3,16,128]{2,1,0:T(8,128)}, u32[]{:S(2)}) copy-start(f32[3,16,128]{2,1,0:T(8,128)} %get-tuple-element.7) | copy-start | bytes 73732
  55.0 0.7 %copy-start = (f32[3,16,128]{2,1,0:T(8,128)S(1)}, f32[3,16,128]{2,1,0:T(8,128)}, u32[]{:S(2)}) copy-start(f32[3,16,128]{2,1,0:T(8,128)} %get-tuple-element.8) | copy-start | bytes 73732
where the time goes:
time: 56.7 us; the launch traced here: 56.3 us
  Pallas kernels  49.6 us (87%)
  local copies, waits for them, and re-layouts  4.16 us (7%)
  between operations  2.59 us (5%)
    pallas_call x1, Pallas kernels, per_device(): pl.pallas_call(functools.partial(kernel, (doms, nb, slots)), out_shape=(s...  49.6 us
    unnamed x8, local copies, waits for them, and re-layouts  4.16 us

commit v1 on v0

--- a/solution.py
+++ b/solution.py
@@ -132,11 +132,9 @@
         total = lax.fori_loop(0, nb, body, jnp.zeros((9 * nb, BLK), F32), unroll=True)
         return unsplit(total, 3 * nb).reshape(3, nb, BLK)
 
-    for b in range(nb):
-        at = slice(b * BLK, (b + 1) * BLK)
-        for k in range(2):
-            for c in range(3):
-                raw_w[(3 * k + c) * nb + b : (3 * k + c) * nb + b + 1, :] = cvw[k, c : c + 1, at]
+    for k in range(2):
+        for c in range(3):
+            raw_w[(3 * k + c) * nb : (3 * k + c + 1) * nb, :] = cvw[pl.ds(2 * nb * c + k, nb, stride=2), :]
     raw_w[6 * nb : 7 * nb, :] = mass[...]
 
     def store_w(k, b, line):
@@ -282,26 +280,36 @@
         place_others(0, features(0)[0])
         place_others(2, features(2)[0])
 
+        def first_of(p):
+            theirs = others_of[other_s[0, p]]
+            return theirs, jnp.dot(turned_own[own_s[0, p]], theirs, preferred_element_type=F32)
+
+        def second_of(p, theirs, logit):
+            weight = jnp.exp2(logit)
+            high = weight.astype(BF16)
+            low = (weight - high.astype(F32)).astype(BF16)
+            lines_of = theirs[0:16, :]
+            pulled = lax.dot_general(
+                jnp.concatenate([lines_of, lines_of], axis=1),
+                jnp.concatenate([high, low], axis=1),
+                (((1,), (1,)), ((), ())),
+                preferred_element_type=F32,
+            )
+            tiles[p] = pulled[0:8, :]
+
         def slots_at(first):
-            for p in [first + u for u in range(UNROLL)]:
-                theirs = others_of[other_s[0, p]]
-                weight = jnp.exp2(jnp.dot(turned_own[own_s[0, p]], theirs, preferred_element_type=F32))
-                high = weight.astype(BF16)
-                low = (weight - high.astype(F32)).astype(BF16)
-                lines_of = theirs[0:16, :]
-                pulled = lax.dot_general(
-                    jnp.concatenate([lines_of, lines_of], axis=1),
-                    jnp.concatenate([high, low], axis=1),
-                    (((1,), (1,)), ((), ())),
-                    preferred_element_type=F32,
-                )
-                tiles[p] = pulled[0:8, :]
+            held_of = [first_of(first + u) for u in range(8)]
+            for g in range(0, 32, 8):
+                later = [first_of(first + g + 8 + u) for u in range(8)] if g + 8 < 32 else []
+                for u in range(8):
+                    second_of(first + g + u, *held_of[u])
+                held_of = later
 
         def body(i, carry):
-            slots_at(i * UNROLL)
+            slots_at(i * 32)
             return carry
 
-        lax.fori_loop(0, slots // UNROLL, body, 0)
+        lax.fori_loop(0, slots // 32, body, 0)
 
         for copy in part_copies:
             copy.wait()
@@ -356,6 +364,7 @@
     smem = pl.BlockSpec(memory_space=pltpu.SMEM)
     dma = pltpu.SemaphoreType.DMA
     shape = jax.ShapeDtypeStruct((3, nb, BLK), F32)
+    weights = cv_weight.transpose(1, 0, 2).reshape(3, 2, nb, BLK).transpose(0, 2, 1, 3).reshape(6 * nb, BLK)
     outs = pl.pallas_call(
         functools.partial(kernel, (doms, nb, slots)),
         out_shape=(shape, shape, shape),
@@ -387,7 +396,7 @@
         compiler_params=pltpu.CompilerParams(collective_id=0, has_side_effects=True),
         name="windows",
     )(
-        positions.reshape(3, nb, BLK), velocities.reshape(3, nb, BLK), inv_mass.reshape(nb, BLK), cv_weight, block_order.reshape(nb, BLK), pair_own,
+        positions.reshape(3, nb, BLK), velocities.reshape(3, nb, BLK), inv_mass.reshape(nb, BLK), weights, block_order.reshape(nb, BLK), pair_own,
         placing(OWN_ROWS, nb), placing(OTHER_ROWS, nb), pair_own, pair_other, pair_count, stiffness, centers[0], accept_row, accept_col,
     )
     return tuple(out.reshape(1, 1, 3, atoms) for out in outs)

time: 56.7 us -> 38.7 us (0.68)
  Pallas kernels: 49.6 us -> 33.1 us
  local copies, waits for them, and re-layouts: 4.16 us -> 2.71 us
    pallas_call x1, Pallas kernels: 49.6 us -> 33.1 us  [per_device(): pl.pallas_call(functools.partial(kernel, (doms, nb, slots)), out_shape=(s...]
    unnamed x8 -> x7, local copies, waits for them, and re-layouts: 4.16 us -> 2.71 us
where the time goes in v1:
time: 38.7 us; the launch traced here: 38.4 us
  Pallas kernels  33.1 us (86%)
  local copies, waits for them, and re-layouts  2.71 us (7%)
  between operations  2.59 us (7%)
    pallas_call x1, Pallas kernels, per_device(): pl.pallas_call(functools.partial(kernel, (doms, nb, slots)), out_shape=(s...  33.1 us
    unnamed x7, local copies, waits for them, and re-layouts  2.71 us

profile of v1, /device:TPU:0, one launch (start us, length us, event | category | flops | bytes accessed | tf_op | source)
XLA Modules:
  0.0 38.4 jit_solution(4836943789264460934)
XLA Ops:
  2.6 33.1 %windows.1 = (f32[3,16,128]{2,1,0:T(8,128)}, f32[3,16,128]{2,1,0:T(8,128)}, f32[3,16,128]{2,1,0:T(8,128)}) custom-call(f32[3,16,128]{2,1,0:T(8,128)} %bitcast.16, f32[3,16,128]{2,1,0:T(8,128)} %bitcast.17, f32[16,128]{1,0:T(8,128)} %bitcast.21, f32[96,128]{1,0:T(8,128)} %bitcast.15, s32[16,128]{1,0:T(8,128)} %bitcast.22, s32[1,64]{1,0:T(1,128)} %own_s.1, ...), custom_call_target="tpu_custom_call" | custom-call | tf_op jit(solution)/shard_map/windows/pallas_call | solution.py:368
  35.7 0.0 copy-start.1
  35.7 1.4 %copy.31 = f32[1,1,3,2048]{3,1,2,0:T(1,128)} copy(f32[1,1,3,2048]{3,1,2,0:T(1,128)} %bitcast.20) | data formatting | bytes 49152
  37.0 0.0 copy-done.1
  37.0 0.0 copy-start
  37.0 0.6 %copy.32 = f32[1,1,3,2048]{3,1,2,0:T(1,128)} copy(f32[1,1,3,2048]{3,1,2,0:T(1,128)S(1)} %bitcast.19) | data formatting | bytes 49152
  37.6 0.1 copy-done
  37.8 0.6 %copy.33 = f32[1,1,3,2048]{3,1,2,0:T(1,128)} copy(f32[1,1,3,2048]{3,1,2,0:T(1,128)S(1)} %bitcast.18) | data formatting | bytes 49152
Async XLA Ops:
  35.7 1.4 %copy-start.1 = (f32[3,16,128]{2,1,0:T(8,128)S(1)}, f32[3,16,128]{2,1,0:T(8,128)}, u32[]{:S(2)}) copy-start(f32[3,16,128]{2,1,0:T(8,128)} %get-tuple-element.7) | copy-start | bytes 73732
  37.0 0.7 %copy-start = (f32[3,16,128]{2,1,0:T(8,128)S(1)}, f32[3,16,128]{2,1,0:T(8,128)}, u32[]{:S(2)}) copy-start(f32[3,16,128]{2,1,0:T(8,128)} %get-tuple-element.8) | copy-start | bytes 73732

commit v2 on v1

v2 whole, which is shorter than its diff:
```python
import functools
import math

import jax
import jax.numpy as jnp
from jax import lax
from jax.experimental import pallas as pl
from jax.experimental.pallas import tpu as pltpu
from jax.sharding import PartitionSpec as P

BLK = 128
SUB = 8
STEPS = 3
PAIR_EPS = 0.015625
DT = 0.1
SCALE = math.sqrt(math.log2(math.e))
GROUP = 8
UNROLL = 64
MESH = pl.DeviceIdType.MESH
F32 = jnp.float32
BF16 = jnp.bfloat16
I32 = jnp.int32


def split2(value):
    high = value.astype(BF16)
    return high, (value - high.astype(F32)).astype(BF16)


def kernel(
    sizes,
    pos, vel, mass, cvw, order, own_row, other_row, count_s, stiff_s, centers_s, arow_s, acol_s,
    out_x, out_v, out_f,
    hot, hot_back, block_of, block_back, raw, raw_w, got_x, got_v, got_aux, aux, parts, prefix, lines_of, turned_of, own_of,
    table_i, table_f, list_s, keep_s, xs, vs, fs, held, half_m, ws,
    sx_send, sx_recv, sv_send, sv_recv, sa_send, sa_recv, halo_send, halo_recv, part_send, part_recv, list_sem, *nears,
):
    doms, nb, slots = sizes
    rows = nb * SUB
    row = lax.axis_index("wrow")
    col = lax.axis_index("wcol")
    me = lax.axis_index("dom")
    row_to = row + 1 - 2 * lax.rem(row, 2)
    col_to = col + 1 - 2 * lax.rem(col, 2)
    partners = [(row_to, col, me), (row, col_to, me), (row_to, col_to, me)]
    others = [(row, col, lax.rem(me + off, doms)) for off in range(1, doms)]

    lines = lax.broadcasted_iota(I32, (SUB, BLK), 0)
    aux[...] = jnp.where(
        lines == 0,
        centers_s[0, 0],
        jnp.where(lines == 1, centers_s[0, 1], arow_s[0, 0].astype(F32)),
    )
    barrier = pltpu.get_barrier_semaphore()
    for target in partners + others:
        pl.semaphore_signal(barrier, inc=1, device_id=target, device_id_type=MESH)
    pl.semaphore_wait(barrier, len(partners) + len(others))

    def exchange(source, target, sends, recvs):
        copies = []
        for at, partner in enumerate(partners):
            copy = pltpu.make_async_remote_copy(
                src_ref=source,
                dst_ref=target.at[at],
                send_sem=sends.at[at],
                recv_sem=recvs.at[at],
                device_id=partner,
                device_id_type=MESH,
            )
            copy.start()
            copies.append(copy)
        return copies

    aux_copies = exchange(aux, got_aux, sa_send, sa_recv)
    x_copies = exchange(pos, got_x, sx_send, sx_recv)
    v_copies = exchange(vel, got_v, sv_send, sv_recv)

    lane_line = lax.broadcasted_iota(I32, (BLK, BLK), 0)

    def spread(low, target):
        for b in range(nb):
            target[:, b * BLK : (b + 1) * BLK] = jnp.where(low[b : b + 1, :] == lane_line, 1.0, 0.0).astype(BF16)

    listed = order[...]
    block_of[...] = lax.div(listed, BLK)
    spread(lax.rem(listed, BLK), hot)

    def moved(source, hots, blocks):
        left = jnp.concatenate(split2(source), axis=1)
        for b in range(0, nb, 2):
            right = hots[:, b * BLK : (b + 2) * BLK]
            got = jnp.dot(left, jnp.concatenate([right, right], axis=0), preferred_element_type=F32)
            for u in range(2):
                home = jnp.broadcast_to(blocks[b + u : b + u + 1, :], (SUB, BLK))
                line = got[0:SUB, u * BLK : (u + 1) * BLK]
                for s in range(1, nb):
                    line = jnp.where(home == s, got[s * SUB : (s + 1) * SUB, u * BLK : (u + 1) * BLK], line)
                yield b + u, line

    raw[...] = jnp.zeros((rows, BLK), F32)
    raw_w[...] = jnp.zeros((rows, BLK), F32)
    for k in range(2):
        for c in range(3):
            raw_w[pl.ds(3 * k + c, nb, stride=SUB), :] = cvw[pl.ds(2 * nb * c + k, nb, stride=2), :]
    raw_w[pl.ds(6, nb, stride=SUB), :] = mass[...]
    three = lines < 3
    for b, line in moved(raw_w[...], hot, block_of):
        ws[0, b] = jnp.where(three, line, 0.0)
        ws[1, b] = jnp.where(three, pltpu.roll(line, SUB - 3, 0), 0.0)
        half_m[b] = jnp.where(three, (0.5 * DT) * jnp.broadcast_to(line[6:7, :], (SUB, BLK)), 0.0)

    slot_lane = lax.broadcasted_iota(I32, (1, slots), 1)
    live = slot_lane < count_s[0]
    owner = jnp.where(live, own_row[...], nb).astype(F32)
    first = lax.broadcasted_iota(I32, (slots, slots), 0)
    second = lax.broadcasted_iota(I32, (slots, slots), 1)
    square = jnp.broadcast_to(owner, (slots, slots))
    unit = jnp.where(first == second, 1.0, 0.0).astype(BF16)
    turned = lax.dot_general(unit, square.astype(BF16), (((1,), (1,)), ((), ())), preferred_element_type=F32)
    ahead = jnp.where((turned == square) & (first < second), 1.0, 0.0)
    earlier = jnp.sum(ahead, axis=0, keepdims=True)
    rank = earlier + jnp.sum(jnp.where(turned < square, 1.0, 0.0), axis=0, keepdims=True)
    chosen_slot = jnp.where(jnp.broadcast_to(rank, (slots, slots)) == first.astype(F32), 1.0, 0.0).astype(BF16)
    list_line = lax.broadcasted_iota(I32, (SUB, slots), 0)
    lists = jnp.where(
        list_line == 0,
        jnp.where(owner < nb, owner, 0.0),
        jnp.where(list_line == 1, other_row[...].astype(F32), jnp.where(earlier > 0.0, 1.0, 0.0)),
    )
    ordered = lax.dot_general(lists.astype(BF16), chosen_slot, (((1,), (1,)), ((), ())), preferred_element_type=F32)
    upto = jnp.sum(jnp.where(turned <= second.astype(F32), 1.0, 0.0), axis=0, keepdims=True)
    some = jnp.sum(jnp.where(turned == second.astype(F32), 1.0, 0.0), axis=0, keepdims=True)
    table_f[...] = jnp.zeros(table_f.shape, F32)
    table_i[...] = jnp.zeros(table_i.shape, I32)
    table_f[:, 0:slots] = ordered
    table_i[:, 0:slots] = jnp.where(list_line == 2, jnp.where(some > 0.0, upto, 0.0), ordered).astype(I32)
    list_copies = [
        pltpu.make_async_copy(table_i, list_s, list_sem.at[0]),
        pltpu.make_async_copy(table_f, keep_s, list_sem.at[1]),
    ]
    for copy in list_copies:
        copy.start()

    for copy in aux_copies:
        copy.wait()
    take_row = jnp.full((SUB, BLK), arow_s[0, 0].astype(F32)) > 0.5
    take_col = jnp.full((SUB, BLK), acol_s[0, 0].astype(F32)) > 0.5
    take_far = jnp.broadcast_to(got_aux[1, 2:3, :], (SUB, BLK)) > 0.5

    def chosen(mine, by_row, by_col, by_both):
        far = jnp.where(take_far, by_both, by_col)
        close = jnp.where(take_row, by_row, mine)
        return jnp.where(take_col, far, close)

    centre = chosen(aux[...], got_aux[0], got_aux[1], got_aux[2])
    centres = [centre[0:1, :], centre[1:2, :]]

    def take_window(source, got):
        for c in range(3):
            for b in range(0, nb, SUB):
                raw[pl.ds(b * SUB + c, SUB, stride=SUB), :] = chosen(
                    source[c, b : b + SUB], got[0, c, b : b + SUB], got[1, c, b : b + SUB], got[2, c, b : b + SUB]
                )

    for copy in x_copies:
        copy.wait()
    take_window(pos, got_x)
    for b, line in moved(raw[...], hot, block_of):
        xs[b] = line

    def take_velocities():
        for copy in list_copies:
            copy.wait()
        for copy in v_copies:
            copy.wait()
        take_window(vel, got_v)
        for b, line in moved(raw[...], hot, block_of):
            vs[b] = line

    def invert():
        block_line = lax.broadcasted_iota(I32, (nb, BLK), 0)
        place = lax.broadcasted_iota(I32, (nb, BLK), 1).astype(F32)
        tops, lows = [], []
        for b in range(nb):
            here = block_of[b : b + 1, :] == block_line
            tops.append(jnp.where(here, float(b), 0.0).astype(BF16))
            lows.append(jnp.where(here, place, 0.0).astype(BF16))
        both = jnp.concatenate([jnp.concatenate(tops, axis=1), jnp.concatenate(lows, axis=1)], axis=0)
        found = lax.dot_general(both, hot[...], (((1,), (1,)), ((), ())), preferred_element_type=F32).astype(I32)
        block_back[...] = found[0:nb]
        spread(found[nb : 2 * nb], hot_back)

    def force(e, meanwhile):
        near = nears[e]
        sums = [jnp.zeros((SUB, BLK), F32), jnp.zeros((SUB, BLK), F32)]
        for b in range(nb):
            x = xs[b]
            near[1, b] = x * SCALE
            for k in range(2):
                sums[k] = sums[k] + ws[k, b] * x
        parts[e, me] = sums[0] + pltpu.roll(sums[1], 3, 0)
        part_copies = []
        for at, target in enumerate(others):
            copy = pltpu.make_async_remote_copy(
                src_ref=parts.at[e, me],
                dst_ref=parts.at[e, me],
                send_sem=part_send.at[e, at],
                recv_sem=part_recv.at[e, at],
                device_id=target,
                device_id_type=MESH,
            )
            copy.start()
            part_copies.append(copy)
        up = pltpu.make_async_remote_copy(
            src_ref=near.at[1, :, 0:3, :],
            dst_ref=near.at[0, :, 0:3, :],
            send_sem=halo_send.at[e, 0],
            recv_sem=halo_recv.at[e, 0],
            device_id=(row, col, lax.rem(me + 1, doms)),
            device_id_type=MESH,
        )
        down = pltpu.make_async_remote_copy(
            src_ref=near.at[1, :, 0:3, :],
            dst_ref=near.at[2, :, 0:3, :],
            send_sem=halo_send.at[e, 1],
            recv_sem=halo_recv.at[e, 1],
            device_id=(row, col, lax.rem(me + doms - 1, doms)),
            device_id_type=MESH,
        )

        @pl.when(me < doms - 1)
        def _():
            up.start()

        @pl.when(me > 0)
        def _():
            down.start()

        def features(slab, b):
            value = near[slab, b]
            high = value.astype(BF16).astype(F32)
            middle = (value - high).astype(BF16).astype(F32)
            kept = high + middle
            square = jnp.where(three, kept * kept, 0.0)
            norm = jnp.broadcast_to(-0.5 * jnp.sum(square, axis=0, keepdims=True), (SUB, BLK))
            one = norm.astype(BF16).astype(F32)
            two = (norm - one).astype(BF16).astype(F32)
            norms = jnp.where(lines == 3, one, jnp.where(lines == 4, two, jnp.where(lines == 5, norm - one - two, 0.0)))
            units = jnp.where((lines >= 3) & (lines < 6), 1.0, 0.0)
            counted = jnp.where(lines == 6, 1.0, 0.0)
            plain = jnp.where(three, high, 0.0)
            fine = jnp.where(three, middle, 0.0)
            theirs = jnp.concatenate([plain + norms + counted, fine + units, plain, fine], axis=0)
            lines_of[slab * nb + b] = theirs[0 : 2 * SUB, :].astype(BF16)
            turned_of[slab * nb + b] = jnp.transpose(theirs).astype(BF16)
            return kept, plain + units, plain + norms, fine

        for b in range(nb):
            kept, top, second_top, fine = features(1, b)
            held[b] = kept
            own_of[b] = jnp.concatenate([top, second_top, fine, fine], axis=0).astype(BF16)

        meanwhile()

        @pl.when(me < doms - 1)
        def _():
            up.wait_send()
            down.wait_recv()

        @pl.when(me > 0)
        def _():
            down.wait_send()
            up.wait_recv()

        for b in range(nb):
            features(0, b)
            features(2, b)

        def ours(p):
            return jnp.clip(list_s[0, p], 0, nb - 1)

        def their(p):
            return jnp.clip(list_s[1, p], 0, 3 * nb - 1)

        def first_of(p):
            return jnp.dot(turned_of[their(p)], own_of[ours(p)], preferred_element_type=F32)

        def second_of(p, carried, logits):
            pieces = [split2(jnp.exp2(logit)) for logit in logits]
            lines_at = [lines_of[their(p + u)] for u in range(2)]
            pulled = jnp.dot(
                jnp.concatenate([jnp.concatenate([line, line], axis=1) for line in lines_at], axis=0),
                jnp.concatenate([jnp.concatenate([pieces[0][h], pieces[1][h]], axis=1) for h in range(2)], axis=0),
                preferred_element_type=F32,
            )
            for u in range(2):
                at = slice(u * BLK, (u + 1) * BLK)
                tile = pulled[2 * u * SUB : (2 * u + 1) * SUB, at] + pulled[(2 * u + 1) * SUB : (2 * u + 2) * SUB, at]
                carried = carried * keep_s[2, p + u] + tile
                prefix[p + u + 1] = carried
            return carried

        def body(i, carried):
            start = i * UNROLL
            ready = [first_of(start + u) for u in range(GROUP)]
            for g in range(0, UNROLL, GROUP):
                later = [first_of(start + g + GROUP + u) for u in range(GROUP)] if g + GROUP < UNROLL else []
                for u in range(0, GROUP, 2):
                    carried = second_of(start + g + u, carried, ready[u : u + 2])
                ready = later
            return carried

        prefix[0] = jnp.zeros((SUB, BLK), F32)
        lax.fori_loop(0, slots // UNROLL, body, jnp.zeros((SUB, BLK), F32))

        for copy in part_copies:
            copy.wait()
        total = parts[e, 0]
        for d in range(1, doms):
            total = total + parts[e, d]
        pulls = []
        for k in range(2):
            collective = jnp.sum(total[3 * k : 3 * k + 3, :], axis=(0, 1), keepdims=True)
            pulls.append(stiff_s[k] * (collective - centres[k]))
        for b in range(nb):
            pulled = prefix[jnp.clip(list_s[2, b], 0, slots)]
            pair = held[b] * jnp.broadcast_to(pulled[6:7, :], (SUB, BLK)) - pulled
            fs[b] = (PAIR_EPS / SCALE) * pair - pulls[0] * ws[0, b] - pulls[1] * ws[1, b]

    force(0, take_velocities)
    for step in range(STEPS):
        for b in range(nb):
            v = vs[b] + half_m[b] * fs[b]
            vs[b] = v
            xs[b] = xs[b] + DT * v
        if step < STEPS - 1:
            force(step + 1, invert if step == 0 else lambda: None)
            for b in range(nb):
                vs[b] = vs[b] + half_m[b] * fs[b]

    def write(source, target):
        for b, line in moved(source[...].reshape(rows, BLK), hot_back, block_back):
            raw[b * SUB : (b + 1) * SUB, :] = line
        for c in range(3):
            target[c] = raw[pl.ds(c, nb, stride=SUB), :]

    def write_state():
        write(xs, out_x)
        write(vs, out_v)

    force(STEPS, write_state)
    write(fs, out_f)
    for c in range(3):
        out_v[c] = out_v[c] + (0.5 * DT) * mass[...] * out_f[c]


def per_device(
    positions, velocities, inv_mass, cv_weight, stiffness, centers, block_order, pair_count, pair_own, pair_other,
    accept_row, accept_col,
):
    atoms = block_order.shape[0]
    nb = atoms // BLK
    slots = pair_own.shape[1]
    doms = lax.axis_size("dom")
    evals = STEPS + 1
    wide = BLK * pl.cdiv(slots, BLK)
    vmem = pl.BlockSpec(memory_space=pltpu.VMEM)
    smem = pl.BlockSpec(memory_space=pltpu.SMEM)
    dma = pltpu.SemaphoreType.DMA
    shape = jax.ShapeDtypeStruct((3, nb, BLK), F32)
    state = pltpu.VMEM((nb, SUB, BLK), F32)
    weights = cv_weight.transpose(1, 0, 2).reshape(3, 2, nb, BLK).transpose(0, 2, 1, 3).reshape(6 * nb, BLK)
    outs = pl.pallas_call(
        functools.partial(kernel, (doms, nb, slots)),
        out_shape=(shape, shape, shape),
        in_specs=[vmem] * 7 + [smem] * 5,
        out_specs=(vmem, vmem, vmem),
        scratch_shapes=[
            pltpu.VMEM((BLK, atoms), BF16),
            pltpu.VMEM((BLK, atoms), BF16),
            pltpu.VMEM((nb, BLK), I32),
            pltpu.VMEM((nb, BLK), I32),
            pltpu.VMEM((nb * SUB, BLK), F32),
            pltpu.VMEM((nb * SUB, BLK), F32),
            pltpu.VMEM((3, 3, nb, BLK), F32),
            pltpu.VMEM((3, 3, nb, BLK), F32),
            pltpu.VMEM((3, SUB, BLK), F32),
            pltpu.VMEM((SUB, BLK), F32),
            pltpu.VMEM((evals, doms, SUB, BLK), F32),
            pltpu.VMEM((slots + 1, SUB, BLK), F32),
            pltpu.VMEM((3 * nb, 2 * SUB, BLK), BF16),
            pltpu.VMEM((3 * nb, BLK, 4 * SUB), BF16),
            pltpu.VMEM((nb, 4 * SUB, BLK), BF16),
            pltpu.VMEM((SUB, wide), I32),
            pltpu.VMEM((SUB, wide), F32),
            pltpu.SMEM((SUB, wide), I32),
            pltpu.SMEM((SUB, wide), F32),
            state, state, state, state, state,
            pltpu.VMEM((2, nb, SUB, BLK), F32),
            dma((3,)), dma((3,)), dma((3,)), dma((3,)), dma((3,)), dma((3,)),
            dma((evals, 2)), dma((evals, 2)), dma((evals, doms)), dma((evals, doms)), dma((2,)),
        ]
        + [pltpu.VMEM((3, nb, SUB, BLK), F32)] * evals,
        compiler_params=pltpu.CompilerParams(collective_id=0, has_side_effects=True),
        name="windows",
    )(
        positions.reshape(3, nb, BLK), velocities.reshape(3, nb, BLK), inv_mass.reshape(nb, BLK), weights, block_order.reshape(nb, BLK), pair_own,
        pair_other, pair_count, stiffness, centers[0], accept_row, accept_col,
    )
    return tuple(out.reshape(1, 1, 3, atoms) for out in outs)


def solution(mesh):
    placed = (
        P("wrow", "wcol", None, "dom"),
        P("wrow", "wcol", None, "dom"),
        P("dom"),
        P(None, None, "dom"),
        P(),
        P("wrow", "wcol", None),
        P("dom"),
        P("dom"),
        P("dom", None),
        P("dom", None),
        P("wrow", "wcol"),
        P("wrow", "wcol"),
    )
    return jax.shard_map(
        per_device,
        mesh=mesh,
        in_specs=placed,
        out_specs=(
            P("wrow", "wcol", None, "dom"),
            P("wrow", "wcol", None, "dom"),
            P("wrow", "wcol", None, "dom"),
        ),
        check_vma=False,
    )
```

time: 38.7 us -> 36.2 us (0.935)
  Pallas kernels: 33.1 us -> 30.6 us
    pallas_call x1, Pallas kernels: 33.1 us -> 30.6 us  [per_device(): pl.pallas_call(functools.partial(kernel, (doms, nb, slots)), out_shape=(s...]
where the time goes in v2:
time: 36.2 us; the launch traced here: 35.9 us
  Pallas kernels  30.6 us (85%)
  local copies, waits for them, and re-layouts  2.71 us (7%)
  between operations  2.59 us (7%)
    pallas_call x1, Pallas kernels, per_device(): pl.pallas_call(functools.partial(kernel, (doms, nb, slots)), out_shape=(s...  30.6 us
    unnamed x7, local copies, waits for them, and re-layouts  2.71 us

profile of v2, /device:TPU:0, one launch (start us, length us, event | category | flops | bytes accessed | tf_op | source)
XLA Modules:
  0.0 35.9 jit_solution(1756975361868266827)
XLA Ops:
  2.6 30.6 %windows.1 = (f32[3,16,128]{2,1,0:T(8,128)}, f32[3,16,128]{2,1,0:T(8,128)}, f32[3,16,128]{2,1,0:T(8,128)}) custom-call(f32[3,16,128]{2,1,0:T(8,128)} %bitcast.19, f32[3,16,128]{2,1,0:T(8,128)} %bitcast.20, f32[16,128]{1,0:T(8,128)} %bitcast.21, f32[96,128]{1,0:T(8,128)} %bitcast.15, s32[16,128]{1,0:T(8,128)} %bitcast.22, s32[1,64]{1,0:T(1,128)} %own_row.1, ...), custom_call_target="tpu_custom_call" | custom-call | tf_op jit(solution)/shard_map/windows/pallas_call | solution.py:373
  33.2 0.0 copy-start.1
  33.2 1.4 %copy.29 = f32[1,1,3,2048]{3,1,2,0:T(1,128)} copy(f32[1,1,3,2048]{3,1,2,0:T(1,128)} %bitcast.18) | data formatting | bytes 49152
  34.6 0.0 copy-done.1
  34.6 0.0 copy-start
  34.6 0.6 %copy.30 = f32[1,1,3,2048]{3,1,2,0:T(1,128)} copy(f32[1,1,3,2048]{3,1,2,0:T(1,128)S(1)} %bitcast.17) | data formatting | bytes 49152
  35.2 0.1 copy-done
  35.3 0.6 %copy.31 = f32[1,1,3,2048]{3,1,2,0:T(1,128)} copy(f32[1,1,3,2048]{3,1,2,0:T(1,128)S(1)} %bitcast.16) | data formatting | bytes 49152
Async XLA Ops:
  33.2 1.4 %copy-start.1 = (f32[3,16,128]{2,1,0:T(8,128)S(1)}, f32[3,16,128]{2,1,0:T(8,128)}, u32[]{:S(2)}) copy-start(f32[3,16,128]{2,1,0:T(8,128)} %get-tuple-element.7) | copy-start | bytes 73732
  34.6 0.7 %copy-start = (f32[3,16,128]{2,1,0:T(8,128)S(1)}, f32[3,16,128]{2,1,0:T(8,128)}, u32[]{:S(2)}) copy-start(f32[3,16,128]{2,1,0:T(8,128)} %get-tuple-element.8) | copy-start | bytes 73732

commit v3 on v2

--- a/solution.py
+++ b/solution.py
@@ -32,8 +32,8 @@
     pos, vel, mass, cvw, order, own_row, other_row, count_s, stiff_s, centers_s, arow_s, acol_s,
     out_x, out_v, out_f,
     hot, hot_back, block_of, block_back, raw, raw_w, got_x, got_v, got_aux, aux, parts, prefix, lines_of, turned_of, own_of,
-    table_i, table_f, list_s, keep_s, xs, vs, fs, held, half_m, ws,
-    sx_send, sx_recv, sv_send, sv_recv, sa_send, sa_recv, halo_send, halo_recv, part_send, part_recv, list_sem, *nears,
+    table_i, table_f, list_s, keep_s, xs, vs, fs, held, half_m, ws, near_w, cross_parts, cross_last,
+    sx_send, sx_recv, sv_send, sv_recv, sa_send, sa_recv, halo_send, halo_recv, part_send, part_recv, list_sem, weight_send, weight_recv, cross_send, cross_recv, *nears,
 ):
     doms, nb, slots = sizes
     rows = nb * SUB
@@ -108,6 +108,65 @@
         ws[0, b] = jnp.where(three, line, 0.0)
         ws[1, b] = jnp.where(three, pltpu.roll(line, SUB - 3, 0), 0.0)
         half_m[b] = jnp.where(three, (0.5 * DT) * jnp.broadcast_to(line[6:7, :], (SUB, BLK)), 0.0)
+    cross = [jnp.zeros((SUB, BLK), F32) for _ in range(3)]
+    for b in range(nb):
+        for k in range(2):
+            shift = DT * half_m[b] * ws[k, b]
+            near_w[1, k, b] = shift
+            for j in range(k, 2):
+                cross[k + j] = cross[k + j] + shift * ws[j, b]
+    cross_parts[me] = cross[0] + pltpu.roll(cross[1], 3, 0)
+    cross_last[me] = cross[2]
+    early = []
+    for at, target in enumerate(others):
+        for which, held_parts in enumerate((cross_parts, cross_last)):
+            copy = pltpu.make_async_remote_copy(
+                src_ref=held_parts.at[me],
+                dst_ref=held_parts.at[me],
+                send_sem=cross_send.at[which, at],
+                recv_sem=cross_recv.at[which, at],
+                device_id=target,
+                device_id_type=MESH,
+            )
+            copy.start()
+            early.append(copy)
+
+    def neighbours(ref, sends, recvs):
+        source = ref.at[1, ..., 0:3, :]
+        return tuple(
+            pltpu.make_async_remote_copy(
+                src_ref=source,
+                dst_ref=ref.at[1 - step, ..., 0:3, :],
+                send_sem=sends.at[at],
+                recv_sem=recvs.at[at],
+                device_id=(row, col, lax.rem(me + doms + step, doms)),
+                device_id_type=MESH,
+            )
+            for at, step in enumerate((1, -1))
+        )
+
+    def send_both(up, down):
+        @pl.when(me < doms - 1)
+        def _():
+            up.start()
+
+        @pl.when(me > 0)
+        def _():
+            down.start()
+
+    def wait_both(up, down):
+        @pl.when(me < doms - 1)
+        def _():
+            up.wait_send()
+            down.wait_recv()
+
+        @pl.when(me > 0)
+        def _():
+            down.wait_send()
+            up.wait_recv()
+
+    weight_halo = neighbours(near_w, weight_send, weight_recv)
+    send_both(*weight_halo)
 
     slot_lane = lax.broadcasted_iota(I32, (1, slots), 1)
     live = slot_lane < count_s[0]
@@ -190,12 +249,12 @@
         block_back[...] = found[0:nb]
         spread(found[nb : 2 * nb], hot_back)
 
-    def force(e, meanwhile):
+    def launch(e):
         near = nears[e]
         sums = [jnp.zeros((SUB, BLK), F32), jnp.zeros((SUB, BLK), F32)]
         for b in range(nb):
             x = xs[b]
-            near[1, b] = x * SCALE
+            near[1, b] = x
             for k in range(2):
                 sums[k] = sums[k] + ws[k, b] * x
         parts[e, me] = sums[0] + pltpu.roll(sums[1], 3, 0)
@@ -211,33 +270,32 @@
             )
             copy.start()
             part_copies.append(copy)
-        up = pltpu.make_async_remote_copy(
-            src_ref=near.at[1, :, 0:3, :],
-            dst_ref=near.at[0, :, 0:3, :],
-            send_sem=halo_send.at[e, 0],
-            recv_sem=halo_recv.at[e, 0],
-            device_id=(row, col, lax.rem(me + 1, doms)),
-            device_id_type=MESH,
-        )
-        down = pltpu.make_async_remote_copy(
-            src_ref=near.at[1, :, 0:3, :],
-            dst_ref=near.at[2, :, 0:3, :],
-            send_sem=halo_send.at[e, 1],
-            recv_sem=halo_recv.at[e, 1],
-            device_id=(row, col, lax.rem(me + doms - 1, doms)),
-            device_id_type=MESH,
-        )
-
-        @pl.when(me < doms - 1)
-        def _():
-            up.start()
-
-        @pl.when(me > 0)
-        def _():
-            down.start()
-
-        def features(slab, b):
-            value = near[slab, b]
+        halo = neighbours(near, halo_send.at[e], halo_recv.at[e])
+        send_both(*halo)
+        return part_copies, halo
+
+    def whole(tile, first):
+        return jnp.sum(tile[first : first + 3, :], axis=(0, 1), keepdims=True)
+
+    def settle(e, part_copies, before, crossed):
+        for copy in part_copies:
+            copy.wait()
+        total = parts[e, 0]
+        for d in range(1, doms):
+            total = total + parts[e, d]
+        pulls = []
+        for k in range(2):
+            collective = whole(total, 3 * k)
+            if before is not None:
+                collective = collective - before[0] * crossed[k] - before[1] * crossed[k + 1]
+            pulls.append(stiff_s[k] * (collective - centres[k][:, 0:1]))
+        return pulls
+
+    def pairs(e, halo, before, meanwhile):
+        near = nears[e]
+
+        def features(slab, b, value):
+            value = value * SCALE
             high = value.astype(BF16).astype(F32)
             middle = (value - high).astype(BF16).astype(F32)
             kept = high + middle
@@ -256,25 +314,19 @@
             return kept, plain + units, plain + norms, fine
 
         for b in range(nb):
-            kept, top, second_top, fine = features(1, b)
+            kept, top, second_top, fine = features(1, b, xs[b])
             held[b] = kept
             own_of[b] = jnp.concatenate([top, second_top, fine, fine], axis=0).astype(BF16)
 
         meanwhile()
 
-        @pl.when(me < doms - 1)
-        def _():
-            up.wait_send()
-            down.wait_recv()
-
-        @pl.when(me > 0)
-        def _():
-            down.wait_send()
-            up.wait_recv()
-
-        for b in range(nb):
-            features(0, b)
-            features(2, b)
+        wait_both(*halo)
+        for b in range(nb):
+            for slab in (0, 2):
+                value = near[slab, b]
+                if before is not None:
+                    value = value - before[0] * near_w[slab, 0, b] - before[1] * near_w[slab, 1, b]
+                features(slab, b, value)
 
         def ours(p):
             return jnp.clip(list_s[0, p], 0, nb - 1)
@@ -313,31 +365,6 @@
         prefix[0] = jnp.zeros((SUB, BLK), F32)
         lax.fori_loop(0, slots // UNROLL, body, jnp.zeros((SUB, BLK), F32))
 
-        for copy in part_copies:
-            copy.wait()
-        total = parts[e, 0]
-        for d in range(1, doms):
-            total = total + parts[e, d]
-        pulls = []
-        for k in range(2):
-            collective = jnp.sum(total[3 * k : 3 * k + 3, :], axis=(0, 1), keepdims=True)
-            pulls.append(stiff_s[k] * (collective - centres[k]))
-        for b in range(nb):
-            pulled = prefix[jnp.clip(list_s[2, b], 0, slots)]
-            pair = held[b] * jnp.broadcast_to(pulled[6:7, :], (SUB, BLK)) - pulled
-            fs[b] = (PAIR_EPS / SCALE) * pair - pulls[0] * ws[0, b] - pulls[1] * ws[1, b]
-
-    force(0, take_velocities)
-    for step in range(STEPS):
-        for b in range(nb):
-            v = vs[b] + half_m[b] * fs[b]
-            vs[b] = v
-            xs[b] = xs[b] + DT * v
-        if step < STEPS - 1:
-            force(step + 1, invert if step == 0 else lambda: None)
-            for b in range(nb):
-                vs[b] = vs[b] + half_m[b] * fs[b]
-
     def write(source, target):
         for b, line in moved(source[...].reshape(rows, BLK), hot_back, block_back):
             raw[b * SUB : (b + 1) * SUB, :] = line
@@ -348,10 +375,56 @@
         write(xs, out_x)
         write(vs, out_v)
 
-    force(STEPS, write_state)
+    def pair_force(b):
+        pulled = prefix[jnp.clip(list_s[2, b], 0, slots)]
+        return (PAIR_EPS / SCALE) * (held[b] * jnp.broadcast_to(pulled[6:7, :], (SUB, BLK)) - pulled)
+
+    part_copies, halo = launch(0)
+    pairs(0, halo, None, take_velocities)
+    before = crossed = None
+    for step in range(STEPS):
+        kick = 1.0 if step == 0 else 2.0
+        for b in range(nb):
+            pair = pair_force(b)
+            fs[b] = pair
+            xs[b] = xs[b] + DT * (vs[b] + kick * half_m[b] * pair)
+        next_copies, halo = launch(step + 1)
+        pulls = settle(step, part_copies, before, crossed)
+        before = [jnp.broadcast_to(kick * pull, (SUB, BLK)) for pull in pulls]
+        for b in range(nb):
+            vs[b] = vs[b] + kick * half_m[b] * (fs[b] - pulls[0] * ws[0, b] - pulls[1] * ws[1, b])
+            xs[b] = xs[b] - before[0] * near_w[1, 0, b] - before[1] * near_w[1, 1, b]
+        before_sum = [kick * pull for pull in pulls]
+
+        def meanwhile():
+            if step == 0:
+                wait_both(*weight_halo)
+                invert()
+            if step == STEPS - 1:
+                write_state()
+
+        if step == 0:
+            for copy in early:
+                copy.wait()
+            total = cross_parts[0]
+            last = cross_last[0]
+            for d in range(1, doms):
+                total = total + cross_parts[d]
+                last = last + cross_last[d]
+            crossed = [whole(total, 0), whole(total, 3), whole(last, 0)]
+        pairs(step + 1, halo, before, meanwhile)
+        before = before_sum
+        part_copies = next_copies
+    pulls = settle(STEPS, part_copies, before, crossed)
+    for b in range(nb):
+        fs[b] = pair_force(b) - pulls[0] * ws[0, b] - pulls[1] * ws[1, b]
     write(fs, out_f)
-    for c in range(3):
-        out_v[c] = out_v[c] + (0.5 * DT) * mass[...] * out_f[c]
+
+
+def finish(mass, x, v, f, out_x, out_v, out_f):
+    out_x[...] = x[...]
+    out_f[...] = f[...]
+    out_v[...] = v[...] + (0.5 * DT) * mass[...][None] * f[...]
 
 
 def per_device(
@@ -397,8 +470,12 @@
             pltpu.SMEM((SUB, wide), F32),
             state, state, state, state, state,
             pltpu.VMEM((2, nb, SUB, BLK), F32),
+            pltpu.VMEM((3, 2, nb, SUB, BLK), F32),
+            pltpu.VMEM((doms, SUB, BLK), F32),
+            pltpu.VMEM((doms, SUB, BLK), F32),
             dma((3,)), dma((3,)), dma((3,)), dma((3,)), dma((3,)), dma((3,)),
             dma((evals, 2)), dma((evals, 2)), dma((evals, doms)), dma((evals, doms)), dma((2,)),
+            dma((2,)), dma((2,)), dma((2, doms)), dma((2, doms)),
         ]
         + [pltpu.VMEM((3, nb, SUB, BLK), F32)] * evals,
         compiler_params=pltpu.CompilerParams(collective_id=0, has_side_effects=True),
@@ -407,6 +484,13 @@
         positions.reshape(3, nb, BLK), velocities.reshape(3, nb, BLK), inv_mass.reshape(nb, BLK), weights, block_order.reshape(nb, BLK), pair_own,
         pair_other, pair_count, stiffness, centers[0], accept_row, accept_col,
     )
+    outs = pl.pallas_call(
+        finish,
+        out_shape=(shape, shape, shape),
+        in_specs=[vmem] * 4,
+        out_specs=(vmem, vmem, vmem),
+        name="finish",
+    )(inv_mass.reshape(nb, BLK), *outs)
     return tuple(out.reshape(1, 1, 3, atoms) for out in outs)
 
 

time: 36.2 us -> 34.8 us (0.961)
  local copies, waits for them, and re-layouts: 2.71 us -> 0 us
  Pallas kernels: 30.6 us -> 31.9 us
    unnamed x7 -> x0, local copies, waits for them, and re-layouts: 2.71 us -> none
    pallas_call x0 -> x1, Pallas kernels: none -> 1.42 us  [per_device(): pl.pallas_call(finish, out_shape=(shape, shape, shape), in_specs=[vmem] *...]
where the time goes in v3:
time: 34.8 us; the launch traced here: 34.5 us
  Pallas kernels  31.9 us (92%)
  between operations  2.58 us (7%)
    pallas_call x1, Pallas kernels, per_device(): pl.pallas_call(functools.partial(kernel, (doms, nb, slots)), out_shape=(s...  30.5 us
    pallas_call x1, Pallas kernels, per_device(): pl.pallas_call(finish, out_shape=(shape, shape, shape), in_specs=[vmem] *...  1.42 us

profile of v3, /device:TPU:0, one launch (start us, length us, event | category | flops | bytes accessed | tf_op | source)
XLA Modules:
  0.0 34.5 jit_solution(11195183210363841156)
XLA Ops:
  2.6 30.5 %windows.1 = (f32[3,16,128]{2,1,0:T(8,128)}, f32[3,16,128]{2,1,0:T(8,128)}, f32[3,16,128]{2,1,0:T(8,128)}) custom-call(f32[3,16,128]{2,1,0:T(8,128)} %bitcast.18, f32[3,16,128]{2,1,0:T(8,128)} %bitcast.19, f32[16,128]{1,0:T(8,128)} %bitcast.16, f32[96,128]{1,0:T(8,128)} %bitcast.15, s32[16,128]{1,0:T(8,128)} %bitcast.20, s32[1,64]{1,0:T(1,128)} %own_row.1, ...), custom_call_target="tpu_custom_call" | custom-call | tf_op jit(solution)/shard_map/windows/pallas_call | solution.py:446
  33.1 1.4 %finish.1 = (f32[3,16,128]{2,1,0:T(8,128)}, f32[3,16,128]{2,1,0:T(8,128)}, f32[3,16,128]{2,1,0:T(8,128)}) custom-call(f32[16,128]{1,0:T(8,128)} %bitcast.17, f32[3,16,128]{2,1,0:T(8,128)} %get-tuple-element.9.x, f32[3,16,128]{2,1,0:T(8,128)} %get-tuple-element.10.v, f32[3,16,128]{2,1,0:T(8,128)} %get-tuple-element.11.f), custom_call_target="tpu_custom_call" | custom-call | tf_op jit(solution)/shard_map/finish/pallas_call | solution.py:487

commit v4 on v3

--- a/solution.py
+++ b/solution.py
@@ -29,8 +29,9 @@
 
 def kernel(
     sizes,
-    pos, vel, mass, cvw, order, own_row, other_row, count_s, stiff_s, centers_s, arow_s, acol_s,
+    pos_h, vel_h, mass_h, cvw_h, order_h, own_h, other_h, count_h, stiff_h, centers_h, arow_h, acol_h,
     out_x, out_v, out_f,
+    pos, vel, mass, cvw, order, own_row, other_row, count_s, stiff_s, centers_s, arow_s, acol_s, in_sem,
     hot, hot_back, block_of, block_back, raw, raw_w, got_x, got_v, got_aux, aux, parts, prefix, lines_of, turned_of, own_of,
     table_i, table_f, list_s, keep_s, xs, vs, fs, held, half_m, ws, near_w, cross_parts, cross_last,
     sx_send, sx_recv, sv_send, sv_recv, sa_send, sa_recv, halo_send, halo_recv, part_send, part_recv, list_sem, weight_send, weight_recv, cross_send, cross_recv, *nears,
@@ -45,15 +46,26 @@
     partners = [(row_to, col, me), (row, col_to, me), (row_to, col_to, me)]
     others = [(row, col, lax.rem(me + off, doms)) for off in range(1, doms)]
 
+    barrier = pltpu.get_barrier_semaphore()
+    for target in partners + others:
+        pl.semaphore_signal(barrier, inc=1, device_id=target, device_id_type=MESH)
+    entered = [
+        pltpu.make_async_copy(source, target, in_sem.at[at])
+        for at, (source, target) in enumerate((
+            (centers_h, centers_s), (arow_h, arow_s), (pos_h, pos), (vel_h, vel), (order_h, order), (cvw_h, cvw), (mass_h, mass),
+            (own_h, own_row), (other_h, other_row), (count_h, count_s), (stiff_h, stiff_s), (acol_h, acol_s),
+        ))
+    ]
+    for copy in entered:
+        copy.start()
+    for copy in entered[0:4]:
+        copy.wait()
     lines = lax.broadcasted_iota(I32, (SUB, BLK), 0)
     aux[...] = jnp.where(
         lines == 0,
         centers_s[0, 0],
         jnp.where(lines == 1, centers_s[0, 1], arow_s[0, 0].astype(F32)),
     )
-    barrier = pltpu.get_barrier_semaphore()
-    for target in partners + others:
-        pl.semaphore_signal(barrier, inc=1, device_id=target, device_id_type=MESH)
     pl.semaphore_wait(barrier, len(partners) + len(others))
 
     def exchange(source, target, sends, recvs):
@@ -75,6 +87,8 @@
     x_copies = exchange(pos, got_x, sx_send, sx_recv)
     v_copies = exchange(vel, got_v, sv_send, sv_recv)
 
+    for copy in entered[4:]:
+        copy.wait()
     lane_line = lax.broadcasted_iota(I32, (BLK, BLK), 0)
 
     def spread(low, target):
@@ -438,7 +452,6 @@
     evals = STEPS + 1
     wide = BLK * pl.cdiv(slots, BLK)
     vmem = pl.BlockSpec(memory_space=pltpu.VMEM)
-    smem = pl.BlockSpec(memory_space=pltpu.SMEM)
     dma = pltpu.SemaphoreType.DMA
     shape = jax.ShapeDtypeStruct((3, nb, BLK), F32)
     state = pltpu.VMEM((nb, SUB, BLK), F32)
@@ -446,9 +459,22 @@
     outs = pl.pallas_call(
         functools.partial(kernel, (doms, nb, slots)),
         out_shape=(shape, shape, shape),
-        in_specs=[vmem] * 7 + [smem] * 5,
+        in_specs=[pl.BlockSpec(memory_space=pl.ANY)] * 12,
         out_specs=(vmem, vmem, vmem),
         scratch_shapes=[
+            pltpu.VMEM((3, nb, BLK), F32),
+            pltpu.VMEM((3, nb, BLK), F32),
+            pltpu.VMEM((nb, BLK), F32),
+            pltpu.VMEM((6 * nb, BLK), F32),
+            pltpu.VMEM((nb, BLK), I32),
+            pltpu.VMEM((1, slots), I32),
+            pltpu.VMEM((1, slots), I32),
+            pltpu.SMEM((1,), I32),
+            pltpu.SMEM((2,), F32),
+            pltpu.SMEM((1, 2), F32),
+            pltpu.SMEM((1, 1), I32),
+            pltpu.SMEM((1, 1), I32),
+            dma((12,)),
             pltpu.VMEM((BLK, atoms), BF16),
             pltpu.VMEM((BLK, atoms), BF16),
             pltpu.VMEM((nb, BLK), I32),

time: 34.8 us -> 34 us (0.977)
  Pallas kernels: 31.9 us -> 31.2 us
    pallas_call x1, Pallas kernels: 30.5 us -> 29.8 us  [per_device(): pl.pallas_call(functools.partial(kernel, (doms, nb, slots)), out_shape=(s...]
where the time goes in v4:
time: 34 us; the launch traced here: 33.8 us
  Pallas kernels  31.2 us (92%)
  between operations  2.58 us (8%)
    pallas_call x1, Pallas kernels, per_device(): pl.pallas_call(functools.partial(kernel, (doms, nb, slots)), out_shape=(s...  29.8 us
    pallas_call x1, Pallas kernels, per_device(): pl.pallas_call(finish, out_shape=(shape, shape, shape), in_specs=[vmem] *...  1.42 us

profile of v4, /device:TPU:0, one launch (start us, length us, event | category | flops | bytes accessed | tf_op | source)
XLA Modules:
  0.0 33.8 jit_solution(14425754902973196914)
XLA Ops:
  2.6 29.8 %windows.1 = (f32[3,16,128]{2,1,0:T(8,128)}, f32[3,16,128]{2,1,0:T(8,128)}, f32[3,16,128]{2,1,0:T(8,128)}) custom-call(f32[3,16,128]{2,1,0:T(8,128)} %bitcast.18, f32[3,16,128]{2,1,0:T(8,128)} %bitcast.19, f32[16,128]{1,0:T(8,128)} %bitcast.16, f32[96,128]{1,0:T(8,128)} %bitcast.15, s32[16,128]{1,0:T(8,128)} %bitcast.20, s32[1,64]{1,0:T(1,128)} %own_h.1, ...), custom_call_target="tpu_custom_call" | custom-call | tf_op jit(solution)/shard_map/windows/pallas_call | solution.py:459
  32.3 1.4 %finish.1 = (f32[3,16,128]{2,1,0:T(8,128)}, f32[3,16,128]{2,1,0:T(8,128)}, f32[3,16,128]{2,1,0:T(8,128)}) custom-call(f32[16,128]{1,0:T(8,128)} %bitcast.17, f32[3,16,128]{2,1,0:T(8,128)} %get-tuple-element.9.x, f32[3,16,128]{2,1,0:T(8,128)} %get-tuple-element.10.v, f32[3,16,128]{2,1,0:T(8,128)} %get-tuple-element.11.f), custom_call_target="tpu_custom_call" | custom-call | tf_op jit(solution)/shard_map/finish/pallas_call | solution.py:513

commit v5 on v4

--- a/solution.py
+++ b/solution.py
@@ -33,8 +33,8 @@
     out_x, out_v, out_f,
     pos, vel, mass, cvw, order, own_row, other_row, count_s, stiff_s, centers_s, arow_s, acol_s, in_sem,
     hot, hot_back, block_of, block_back, raw, raw_w, got_x, got_v, got_aux, aux, parts, prefix, lines_of, turned_of, own_of,
-    table_i, table_f, list_s, keep_s, xs, vs, fs, held, half_m, ws, near_w, cross_parts, cross_last,
-    sx_send, sx_recv, sv_send, sv_recv, sa_send, sa_recv, halo_send, halo_recv, part_send, part_recv, list_sem, weight_send, weight_recv, cross_send, cross_recv, *nears,
+    table_i, table_f, list_s, keep_s, xs, vs, fs, held, half_m, ws, near_w, cross_parts, cross_last, done, given,
+    sx_send, sx_recv, sv_send, sv_recv, sa_send, sa_recv, halo_send, halo_recv, part_send, part_recv, list_sem, weight_send, weight_recv, cross_send, cross_recv, home_send, home_recv, *nears,
 ):
     doms, nb, slots = sizes
     rows = nb * SUB
@@ -44,7 +44,15 @@
     row_to = row + 1 - 2 * lax.rem(row, 2)
     col_to = col + 1 - 2 * lax.rem(col, 2)
     partners = [(row_to, col, me), (row, col_to, me), (row_to, col_to, me)]
-    others = [(row, col, lax.rem(me + off, doms)) for off in range(1, doms)]
+    odd = lax.rem(me, 2)
+
+    def row_at(slab):
+        return row + (row_to - row) * lax.rem(me + slab, 2)
+
+    others = []
+    for off in range(1, doms):
+        slab = lax.rem(me + off, doms)
+        others.append((row_at(slab), col, slab))
 
     barrier = pltpu.get_barrier_semaphore()
     for target in partners + others:
@@ -52,19 +60,21 @@
     entered = [
         pltpu.make_async_copy(source, target, in_sem.at[at])
         for at, (source, target) in enumerate((
-            (centers_h, centers_s), (arow_h, arow_s), (pos_h, pos), (vel_h, vel), (order_h, order), (cvw_h, cvw), (mass_h, mass),
-            (own_h, own_row), (other_h, other_row), (count_h, count_s), (stiff_h, stiff_s), (acol_h, acol_s),
+            (centers_h, centers_s), (arow_h, arow_s), (acol_h, acol_s), (pos_h, pos), (vel_h, vel), (order_h, order), (cvw_h, cvw), (mass_h, mass),
+            (own_h, own_row), (other_h, other_row), (count_h, count_s), (stiff_h, stiff_s),
         ))
     ]
     for copy in entered:
         copy.start()
-    for copy in entered[0:4]:
+    for copy in entered[0:5]:
         copy.wait()
     lines = lax.broadcasted_iota(I32, (SUB, BLK), 0)
     aux[...] = jnp.where(
         lines == 0,
         centers_s[0, 0],
-        jnp.where(lines == 1, centers_s[0, 1], arow_s[0, 0].astype(F32)),
+        jnp.where(
+            lines == 1, centers_s[0, 1], jnp.where(lines == 2, arow_s[0, 0].astype(F32), acol_s[0, 0].astype(F32))
+        ),
     )
     pl.semaphore_wait(barrier, len(partners) + len(others))
 
@@ -87,7 +97,7 @@
     x_copies = exchange(pos, got_x, sx_send, sx_recv)
     v_copies = exchange(vel, got_v, sv_send, sv_recv)
 
-    for copy in entered[4:]:
+    for copy in entered[5:]:
         copy.wait()
     lane_line = lax.broadcasted_iota(I32, (BLK, BLK), 0)
 
@@ -153,7 +163,7 @@
                 dst_ref=ref.at[1 - step, ..., 0:3, :],
                 send_sem=sends.at[at],
                 recv_sem=recvs.at[at],
-                device_id=(row, col, lax.rem(me + doms + step, doms)),
+                device_id=(row_to, col, lax.rem(me + doms + step, doms)),
                 device_id_type=MESH,
             )
             for at, step in enumerate((1, -1))
@@ -217,10 +227,16 @@
     for copy in aux_copies:
         copy.wait()
     take_row = jnp.full((SUB, BLK), arow_s[0, 0].astype(F32)) > 0.5
-    take_col = jnp.full((SUB, BLK), acol_s[0, 0].astype(F32)) > 0.5
+    swap = jnp.full((SUB, BLK), odd) > 0
+    col_flag = jnp.where(
+        swap, jnp.broadcast_to(got_aux[0, 3:4, :], (SUB, BLK)), jnp.broadcast_to(aux[3:4, :], (SUB, BLK))
+    )
+    take_col = col_flag > 0.5
     take_far = jnp.broadcast_to(got_aux[1, 2:3, :], (SUB, BLK)) > 0.5
 
     def chosen(mine, by_row, by_col, by_both):
+        mine, by_row = jnp.where(swap, by_row, mine), jnp.where(swap, mine, by_row)
+        by_col, by_both = jnp.where(swap, by_both, by_col), jnp.where(swap, by_col, by_both)
         far = jnp.where(take_far, by_both, by_col)
         close = jnp.where(take_row, by_row, mine)
         return jnp.where(take_col, far, close)
@@ -379,15 +395,31 @@
         prefix[0] = jnp.zeros((SUB, BLK), F32)
         lax.fori_loop(0, slots // UNROLL, body, jnp.zeros((SUB, BLK), F32))
 
-    def write(source, target):
+    def write(source, at):
         for b, line in moved(source[...].reshape(rows, BLK), hot_back, block_back):
             raw[b * SUB : (b + 1) * SUB, :] = line
         for c in range(3):
-            target[c] = raw[pl.ds(c, nb, stride=SUB), :]
+            done[at, c] = raw[pl.ds(c, nb, stride=SUB), :]
+        copy = pltpu.make_async_remote_copy(
+            src_ref=done.at[at],
+            dst_ref=given.at[at],
+            send_sem=home_send.at[at],
+            recv_sem=home_recv.at[at],
+            device_id=partners[0],
+            device_id_type=MESH,
+        )
+
+        @pl.when(odd == 1)
+        def _():
+            copy.start()
+
+        return copy
+
+    homes = []
 
     def write_state():
-        write(xs, out_x)
-        write(vs, out_v)
+        homes.append(write(xs, 0))
+        homes.append(write(vs, 1))
 
     def pair_force(b):
         pulled = prefix[jnp.clip(list_s[2, b], 0, slots)]
@@ -432,7 +464,18 @@
     pulls = settle(STEPS, part_copies, before, crossed)
     for b in range(nb):
         fs[b] = pair_force(b) - pulls[0] * ws[0, b] - pulls[1] * ws[1, b]
-    write(fs, out_f)
+    homes.append(write(fs, 2))
+
+    @pl.when(odd == 0)
+    def _():
+        for at, out in enumerate((out_x, out_v, out_f)):
+            out[...] = done[at]
+
+    @pl.when(odd == 1)
+    def _():
+        for copy, at, out in zip(homes, range(3), (out_x, out_v, out_f)):
+            copy.wait()
+            out[...] = given[at]
 
 
 def finish(mass, x, v, f, out_x, out_v, out_f):
@@ -499,9 +542,11 @@
             pltpu.VMEM((3, 2, nb, SUB, BLK), F32),
             pltpu.VMEM((doms, SUB, BLK), F32),
             pltpu.VMEM((doms, SUB, BLK), F32),
+            pltpu.VMEM((3, 3, nb, BLK), F32),
+            pltpu.VMEM((3, 3, nb, BLK), F32),
             dma((3,)), dma((3,)), dma((3,)), dma((3,)), dma((3,)), dma((3,)),
             dma((evals, 2)), dma((evals, 2)), dma((evals, doms)), dma((evals, doms)), dma((2,)),
-            dma((2,)), dma((2,)), dma((2, doms)), dma((2, doms)),
+            dma((2,)), dma((2,)), dma((2, doms)), dma((2, doms)), dma((3,)), dma((3,)),
         ]
         + [pltpu.VMEM((3, nb, SUB, BLK), F32)] * evals,
         compiler_params=pltpu.CompilerParams(collective_id=0, has_side_effects=True),

time: 34 us -> 32.9 us (0.968)
  Pallas kernels: 31.2 us -> 30.1 us
    pallas_call x1, Pallas kernels: 29.8 us -> 28.6 us  [per_device(): pl.pallas_call(functools.partial(kernel, (doms, nb, slots)), out_shape=(s...]
where the time goes in v5:
time: 32.9 us; the launch traced here: 32.6 us
  Pallas kernels  30.1 us (91%)
  between operations  2.58 us (8%)
    pallas_call x1, Pallas kernels, per_device(): pl.pallas_call(functools.partial(kernel, (doms, nb, slots)), out_shape=(s...  28.6 us
    pallas_call x1, Pallas kernels, per_device(): pl.pallas_call(finish, out_shape=(shape, shape, shape), in_specs=[vmem] *...  1.42 us

profile of v5, /device:TPU:0, one launch (start us, length us, event | category | flops | bytes accessed | tf_op | source)
XLA Modules:
  0.0 32.6 jit_solution(1815008221916606278)
XLA Ops:
  2.6 28.6 %windows.1 = (f32[3,16,128]{2,1,0:T(8,128)}, f32[3,16,128]{2,1,0:T(8,128)}, f32[3,16,128]{2,1,0:T(8,128)}) custom-call(f32[3,16,128]{2,1,0:T(8,128)} %bitcast.18, f32[3,16,128]{2,1,0:T(8,128)} %bitcast.19, f32[16,128]{1,0:T(8,128)} %bitcast.16, f32[96,128]{1,0:T(8,128)} %bitcast.15, s32[16,128]{1,0:T(8,128)} %bitcast.20, s32[1,64]{1,0:T(1,128)} %own_h.1, ...), custom_call_target="tpu_custom_call" | custom-call | tf_op jit(solution)/shard_map/windows/pallas_call | solution.py:502
  31.2 1.4 %finish.1 = (f32[3,16,128]{2,1,0:T(8,128)}, f32[3,16,128]{2,1,0:T(8,128)}, f32[3,16,128]{2,1,0:T(8,128)}) custom-call(f32[16,128]{1,0:T(8,128)} %bitcast.17, f32[3,16,128]{2,1,0:T(8,128)} %get-tuple-element.9.x, f32[3,16,128]{2,1,0:T(8,128)} %get-tuple-element.10.v, f32[3,16,128]{2,1,0:T(8,128)} %get-tuple-element.11.f), custom_call_target="tpu_custom_call" | custom-call | tf_op jit(solution)/shard_map/finish/pallas_call | solution.py:558
